TPU v7x, 256 devices: a whole 4x4x8 slice. The times are simulated.
256 devices in a mesh: seq: 16 (over z, core), tp: 16 (over y, x).
Axes of the slice: x: 4, y: 4, z: 8, core: 2. Of those that a mesh axis runs over, the one named last changes fastest.
Arguments:
- latents: bfloat16 [16, 8192, 512], P(None, ('seq', 'tp')), may hold values from -6 to 6
- rotary_rows: bfloat16 [16, 8192, 64], P(None, ('seq', 'tp')), may hold values from -6 to 6
- latent_gain: float32 [512], replicated, may hold values from 0.25 to 1.75
- key_up: bfloat16 [512, 16, 128], P(None, 'tp'), may hold values from -0.25 to 0.25
- value_up: bfloat16 [512, 16, 128], P(None, 'tp'), may hold values from -0.25 to 0.25
Outputs:
- decode_keys: bfloat16 [16, 16, 192, 8192], P('seq', 'tp')
- decode_values: bfloat16 [16, 8192, 16, 128], P('seq', None, 'tp')
All inputs are finite; a program needn't handle non-finite values.
Results may differ from a plain program's by a relative error of at most 0.0049.
Values may be sent and summed in bfloat16 or wider, within the bound.
A program may use at most 64 MiB of HBM per device.

v0:
```python
import jax
import jax.numpy as jnp
from jax import lax
from jax.sharding import PartitionSpec as P


def in_one_piece(arrays, axis, split_dim, concat_dim, along):
    both = jnp.concatenate(arrays, axis=along)
    filled, at, done = (
        lax.all_to_all(both, axis, split_axis=split_dim, concat_axis=concat_dim, tiled=True),
        0,
        [],
    )
    for a in arrays:
        done.append(lax.slice_in_dim(filled, at, at + a.shape[along], axis=along))
        at += a.shape[along]
    return tuple(done)


def in_one_piece_2(arrays, axis, dim, along):
    both = jnp.concatenate(arrays, axis=along)
    filled, at, done = (lax.all_gather(both, axis, axis=dim, tiled=True), 0, [])
    for a in arrays:
        done.append(lax.slice_in_dim(filled, at, at + a.shape[along], axis=along))
        at += a.shape[along]
    return tuple(done)


def expand_rows(rows, rotary, key_up, value_up):
    wide_keys = jnp.einsum(
        "btr,rhk->bthk", rows, key_up, preferred_element_type=jnp.float32
    ).astype(jnp.bfloat16)
    shared = rotary[:, :, None]
    wide_values = jnp.einsum(
        "btr,rhk->bthk", rows, value_up, preferred_element_type=jnp.float32
    ).astype(jnp.bfloat16)
    return (jnp.concatenate([wide_keys, shared], axis=-1), wide_values)


def root_norm(vectors, row_gain):
    return (
        vectors * lax.rsqrt(jnp.mean(vectors * vectors, axis=-1, keepdims=True) + 1e-06) * row_gain
    )


def shards(latents, rotary_rows, latent_gain, key_up, value_up):
    rows_ready = root_norm(latents.astype(jnp.float32), latent_gain).astype(jnp.bfloat16)
    rows_moved, rotary_moved = in_one_piece((rows_ready, rotary_rows), "seq", 0, 1, 2)
    rows_cut = rows_moved.reshape(
        rows_moved.shape[0], lax.axis_size("seq"), -1, rows_moved.shape[2]
    )
    rotary_cut = rotary_moved.reshape(
        rotary_moved.shape[0], lax.axis_size("seq"), -1, rotary_moved.shape[2]
    )
    rows_joined, rotary_joined = in_one_piece_2((rows_cut, rotary_cut), "tp", 2, 3)
    rows_whole = rows_joined.reshape(rows_joined.shape[0], -1, rows_joined.shape[3])
    rotary_whole = rotary_joined.reshape(rotary_joined.shape[0], -1, rotary_joined.shape[3])
    decode_keys, decode_values = expand_rows(rows_whole, rotary_whole, key_up, value_up)
    decode_keys = jnp.transpose(decode_keys, (0, 2, 3, 1))
    return (decode_keys, decode_values)


def solution(mesh):
    return jax.shard_map(
        shards,
        mesh=mesh,
        in_specs=(
            P(None, ("seq", "tp"), None),
            P(None, ("seq", "tp"), None),
            P(),
            P(None, "tp", None),
            P(None, "tp", None),
        ),
        out_specs=(P("seq", "tp", None, None), P("seq", None, "tp", None)),
        check_vma=False,
    )
```

profile of v0, /device:TPU:1, one launch (start us, length us, event | category | flops | bytes accessed | tf_op | source)
XLA Modules:
  0.0 152.4 jit_solution(16020864475576484220)
XLA Ops:
  7.2 0.0 copy-start
  7.2 0.0 all-gather.2.cloned.1.call-start
  7.2 1.2 fusion.2
  8.5 1.2 fusion.4
  9.7 1.0 pad_maximum_fusion
  10.7 30.0 %all_to_all.12 = bf16[16,32,576]{2,1,0:T(8,128)(2,1)S(1)} all-to-all(bf16[16,32,576]{2,1,0:T(8,128)(2,1)S(1)} %pad_maximum_fusion), channel_id=1, replica_groups=mesh['seq'=16,'tp'=16] {'seq'}, dimensions={0} | all-to-all | bytes 1179648 | tf_op jit(solution)/shard_map/all_to_all | solution.py:10
  40.7 0.9 pad_maximum_fusion.1
  41.6 0.0 all-gather.2.cloned.1.call-update
  41.7 82.0 %all-gather.2.cloned.1.call-done = bf16[1,16,512,576]{3,2,1,0:T(8,128)(2,1)} async-done(((bf16[1,16,32,576]{3,2,1,0:T(8,128)(2,1)}), bf16[1,16,512,576]{3,2,1,0:T(8,128)(2,1)}) %all-gather.2.cloned.1.call-update) | async-done | bytes 9437200 | tf_op jit(solution)/shard_map/all_gather | solution.py:22
  123.7 0.0 slice-start
  123.7 1.6 %slice-done = bf16[1,16,512,64]{3,2,1,0:T(8,128)(2,1)S(1)} async-done(((bf16[1,16,512,576]{3,2,1,0:T(8,128)(2,1)}), bf16[1,16,512,64]{3,2,1,0:T(8,128)(2,1)S(1)}, s32[]{:S(2)}) %slice-start) | async-done | bytes 1048600 | tf_op jit(solution)/shard_map/slice | solution.py:24
  125.3 0.8 copy.10
  126.1 7.4 %slice.18 = bf16[1,16,512,512]{3,2,1,0:T(8,128)(2,1)} slice(bf16[1,16,512,576]{3,2,1,0:T(8,128)(2,1)} %all-gather.2.cloned.1.call-done), slice={[0:1], [0:16], [0:512], [0:512]} | slice | bytes 16777216 | tf_op jit(solution)/shard_map/slice | solution.py:24
  133.5 0.0 copy-done
  133.5 0.0 copy-start.1
  133.5 0.0 copy-start.2
  133.5 6.4 %fusion = bf16[1,8192,1,128]{1,3,2,0:T(8,128)(2,1)S(1)} fusion(bf16[8192,512]{1,0:T(8,128)(2,1)} %bitcast.19, bf16[512,1,128]{2,0,1:T(8,128)(2,1)S(1)} %copy-done), kind=kOutput, calls=%fused_computation.2 | convolution fusion | flops 1074790400 | bytes 10616832 | tf_op jit(solution)/shard_map/btr,rhk->bthk/dot_general | solution.py:30
  139.9 0.0 copy-done.1
  139.9 0.0 copy-done.2
  139.9 3.7 %fusion.1 = bf16[1,8192,1,128]{3,1,2,0:T(8,128)(2,1)} fusion(bf16[8192,512]{1,0:T(8,128)(2,1)S(1)} %bitcast.20, bf16[512,1,128]{2,0,1:T(8,128)(2,1)S(1)} %copy-done.2), kind=kOutput, calls=%fused_computation.3 | convolution fusion | flops 1074790400 | bytes 10616832 | tf_op jit(solution)/shard_map/btr,rhk->bthk/dot_general | solution.py:34
  143.6 1.9 %maximum_bitcast_fusion = bf16[1,1,192,8192]{3,2,1,0:T(8,128)(2,1)} fusion(bf16[1,8192,1,64]{1,3,2,0:T(8,128)(2,1)S(1)} %copy.10, bf16[1,8192,1,128]{1,3,2,0:T(8,128)(2,1)S(1)} %fusion), kind=kLoop, calls=%fused_computation.4 | loop fusion | flops 6291456 | bytes 6291456 | tf_op jit(solution)/shard_map/transpose | solution.py:59
  (3 shorter events, 0.1 us)
Async XLA Ops:
  7.2 126.4 %copy-start = (bf16[512,1,128]{2,0,1:T(8,128)(2,1)S(1)}, bf16[512,1,128]{2,0,1:T(8,128)(2,1)}, u32[]{:S(2)}) copy-start(bf16[512,1,128]{2,0,1:T(8,128)(2,1)} %param.8) | copy-start | bytes 393220
  7.2 116.5 %all-gather.2.cloned.1.call-start = ((), (), s32[]{:S(2)}) async-start(), calls=%async_computation.1 | async-start | bytes 11141120 | tf_op jit(solution)/shard_map/all_gather | solution.py:22
  123.7 1.6 %slice-start = ((bf16[1,16,512,576]{3,2,1,0:T(8,128)(2,1)}), bf16[1,16,512,64]{3,2,1,0:T(8,128)(2,1)S(1)}, s32[]{:S(2)}) async-start(bf16[1,16,512,576]{3,2,1,0:T(8,128)(2,1)} %all-gather.2.cloned.1.call-done), calls=%async_computation.2 | async-start | bytes 4194304 | tf_op jit(solution)/shard_map/slice | solution.py:24
  133.5 6.4 %copy-start.1 = (bf16[1,16,512,512]{3,2,1,0:T(8,128)(2,1)S(1)}, bf16[1,16,512,512]{3,2,1,0:T(8,128)(2,1)}, u32[]{:S(2)}) copy-start(bf16[1,16,512,512]{3,2,1,0:T(8,128)(2,1)} %slice.18) | copy-start | bytes 25165828
  133.5 6.4 %copy-start.2 = (bf16[512,1,128]{2,0,1:T(8,128)(2,1)S(1)}, bf16[512,1,128]{2,0,1:T(8,128)(2,1)}, u32[]{:S(2)}) copy-start(bf16[512,1,128]{2,0,1:T(8,128)(2,1)} %param.9) | copy-start | bytes 393220
Sparse Core Ops, SparseCore 0:
  41.8 81.8 all-gather.1
where the time goes:
time: 153 us; the launch traced here: 152 us
  waiting for transfers between devices  82 us (54%)
  blocking collectives  30 us (20%)
  between operations  14.1 us (9%)
  matrix products  10 us (7%)
  local copies, waits for them, and re-layouts  9.92 us (6%)
  other arithmetic  6.3 us (4%)
    all_gather x1, waiting for transfers between devices, in_one_piece_2(): filled, at, done = (lax.all_gather(both, axis, axis=dim, tiled=True), 0, [])  82 us
    all_to_all x1, blocking collectives, in_one_piece(): lax.all_to_all(both, axis, split_axis=split_dim, concat_axis=concat_dim,...  30 us
    slice x3, local copies, waits for them, and re-layouts, in_one_piece_2(): done.append(lax.slice_in_dim(filled, at, at + a.shape[along], axis=along))  9.04 us
    dot_general x1, matrix products, expand_rows(): jnp.einsum('btr,rhk->bthk', rows, key_up, preferred_element_type=jnp.floa...  6.37 us
    dot_general x1, matrix products, expand_rows(): jnp.einsum('btr,rhk->bthk', rows, value_up, preferred_element_type=jnp.fl...  3.66 us
  transfers between devices with their start and end apart: 1, of which 1 were waited for; matrix products, arithmetic and copies ran while one was open for 0% of the time, Pallas kernels for 0%

commit v1 on v0

v1 whole, which is shorter than its diff:
```python
import functools

import jax
import jax.numpy as jnp
from jax import lax
from jax.experimental import pallas as pl
from jax.experimental.pallas import tpu as pltpu
from jax.sharding import PartitionSpec as P

SEQ, TP, RING = 16, 16, 4
ROWS, WIDTH, ROT, HEAD = 32, 512, 64, 128
PACKED = ROWS * WIDTH // 128 + ROWS * ROT // 128
CHUNKS = WIDTH // 128
FLAT = CHUNKS * ROWS
UNIT = TP * ROWS
D1, D2, D3, D4 = 1, 2, 3, 5


def kernel(
    lat_ref, rot_ref, gain_ref, wk_ref, wv_ref, keys_ref, values_ref,
    own, held, weights, spread, send_sem, recv_sem,
):
    seq, tp = lax.axis_index("seq"), lax.axis_index("tp")
    z, core = seq // 2, seq % 2
    y, x = tp // RING, tp % RING

    def seq_of(n):
        k = n // 2
        dz = ((k + 1) // 2) * (1 - 2 * ((k + 1) % 2))
        return ((z + dz + 8) % 8) * 2 + (core + n) % 2

    def tp_of(n, p, q):
        first_y = n % 2
        dy = first_y * p + (1 - first_y) * q
        dx = first_y * q + (1 - first_y) * p
        return ((y + dy + RING) % RING) * RING + (x + dx + RING) % RING

    barrier = pltpu.get_barrier_semaphore()

    def greet(n, _):
        pl.semaphore_signal(barrier, inc=1, device_id=(seq_of(n), tp))
        return _

    lax.fori_loop(1, SEQ, greet, 0)
    for p, q in ((1, 0), (-1, 0), (0, 1), (0, -1)):
        pl.semaphore_signal(barrier, inc=1, device_id=(seq, tp_of(0, p, q)))

    def prepare(s, _):
        rows = lat_ref[s].astype(jnp.float32)
        scale = lax.rsqrt(jnp.mean(rows * rows, axis=-1, keepdims=True) + 1e-06)
        ready = (rows * scale * gain_ref[...]).astype(jnp.bfloat16)
        for c in range(CHUNKS):
            own[s, c * ROWS : (c + 1) * ROWS, :] = ready[:, c * 128 : (c + 1) * 128]
        rot = rot_ref[s]
        own[s, FLAT:PACKED, :] = jnp.concatenate(
            [rot[: ROWS // 2], rot[ROWS // 2 :]], axis=-1
        )
        return _

    lax.fori_loop(0, SEQ, prepare, 0)
    held[seq * TP + tp] = own[seq]
    weights[:, :HEAD] = wk_ref[...]
    weights[:, HEAD:] = wv_ref[...]
    row = lax.broadcasted_iota(jnp.int32, (64, 128), 0)
    lane = lax.broadcasted_iota(jnp.int32, (64, 128), 1)
    for h in range(2):
        at = (row // 16) * 32 + h * 16 + row % 16
        spread[h] = (at == lane).astype(jnp.float32).astype(jnp.bfloat16)

    pl.semaphore_wait(barrier, SEQ - 1 + 4)

    def scatter(n, _):
        pltpu.make_async_remote_copy(
            src_ref=own.at[seq_of(n)],
            dst_ref=held.at[seq * TP + tp],
            send_sem=send_sem,
            recv_sem=recv_sem.at[seq * TP + tp],
            device_id=(seq_of(n), tp),
        ).start()
        return _

    lax.fori_loop(1, SEQ, scatter, 0)

    def copy_of(slot, target):
        return pltpu.make_async_remote_copy(
            src_ref=held.at[slot],
            dst_ref=held.at[slot],
            send_sem=send_sem,
            recv_sem=recv_sem.at[slot],
            device_id=(seq, target),
        )

    def slot_of(n, p, q):
        return seq_of(n) * TP + tp_of(n, p, q)

    def arrive(n, p, q):
        copy_of(slot_of(n, p, q), tp_of(n, 1, 0)).wait_recv()

    def send(n, p, q, dp, dq):
        copy_of(slot_of(n, p, q), tp_of(n, dp, dq)).start()

    def when(n, low=0):
        return pl.when((n >= low) & (n < SEQ))

    def step(it, carry):
        n0, n1, n2, n3, n4 = it, it - D1, it - D2, it - D3, it - D4

        @when(n0, 1)
        def _():
            arrive(n0, 0, 0)

        @when(n0)
        def _():
            send(n0, 0, 0, 1, 0)
            send(n0, 0, 0, -1, 0)
            send(n0, 0, 0, 0, 1)
            send(n0, 0, 0, 0, -1)

        @when(n1)
        def _():
            way = 1 - 2 * ((n1 // 2) % 2)
            arrive(n1, 0 - way, 0)
            send(n1, 0 - way, 0, way, 0)
            send(n1, 0 - way, 0, 0, 1)
            send(n1, 0 - way, 0, 0, -1)
            arrive(n1, way, 0)
            send(n1, way, 0, 0, 1)
            send(n1, way, 0, 0, -1)

        @when(n2)
        def _():
            arrive(n2, 2, 0)
            send(n2, 2, 0, 0, 1)
            send(n2, 2, 0, 0, -1)

        @when(n3)
        def _():
            arrive(n3, 0, -1)
            send(n3, 0, -1, 0, 1)
            arrive(n3, -1, 1)
            send(n3, -1, 1, 0, -1)
            arrive(n3, 1, -1)
            send(n3, 1, -1, 0, 1)
            arrive(n3, 2, 1)
            send(n3, 2, 1, 0, -1)

        @when(n4)
        def _():
            arrive(n4, 0, 1)
            arrive(n4, 1, 1)
            arrive(n4, -1, -1)
            arrive(n4, 2, -1)
            for p in (0, -1, 1, 2):
                arrive(n4, p, 2)
            u = seq_of(n4)
            for q in range(TP // 4):
                block = held[pl.ds(u * TP + 4 * q, 4)]
                rows = jnp.concatenate(
                    [
                        block[:, c * ROWS : (c + 1) * ROWS, :].reshape(4 * ROWS, 128)
                        for c in range(CHUNKS)
                    ],
                    axis=-1,
                )
                wide = jnp.dot(rows, weights[...], preferred_element_type=jnp.float32)
                at = pl.multiple_of(u * UNIT + q * 128, 128)
                values_ref[pl.ds(at, 128), :] = wide[:, HEAD:].astype(jnp.bfloat16)
                keys_ref[:HEAD, pl.ds(at, 128)] = wide[:, :HEAD].T.astype(jnp.bfloat16)
                rot = block[:, FLAT:, :].reshape(64, 128).astype(jnp.float32).T
                rot = rot.astype(jnp.bfloat16)
                turned = jnp.dot(
                    rot[:ROT], spread[0], preferred_element_type=jnp.float32
                ) + jnp.dot(rot[ROT:], spread[1], preferred_element_type=jnp.float32)
                keys_ref[HEAD:, pl.ds(at, 128)] = turned.astype(jnp.bfloat16)

        return carry

    lax.fori_loop(0, SEQ + D4, step, 0)
    sent = SEQ * TP - 1
    pltpu.make_async_copy(held.at[pl.ds(0, sent)], held.at[pl.ds(0, sent)], send_sem).wait()


def shards(latents, rotary_rows, latent_gain, key_up, value_up):
    length = SEQ * UNIT
    vmem = pl.BlockSpec(memory_space=pltpu.VMEM)
    keys, values = pl.pallas_call(
        kernel,
        out_shape=(
            jax.ShapeDtypeStruct((HEAD + ROT, length), jnp.bfloat16),
            jax.ShapeDtypeStruct((length, HEAD), jnp.bfloat16),
        ),
        in_specs=[vmem] * 5,
        out_specs=(vmem, vmem),
        scratch_shapes=[
            pltpu.VMEM((SEQ, PACKED, 128), jnp.bfloat16),
            pltpu.VMEM((SEQ * TP, PACKED, 128), jnp.bfloat16),
            pltpu.VMEM((WIDTH, 2 * HEAD), jnp.bfloat16),
            pltpu.VMEM((2, 64, 128), jnp.bfloat16),
            pltpu.SemaphoreType.DMA,
            pltpu.SemaphoreType.DMA((SEQ * TP,)),
        ],
        compiler_params=pltpu.CompilerParams(collective_id=0, has_side_effects=True),
        name="gather_and_expand",
    )(
        latents,
        rotary_rows,
        latent_gain.reshape(1, WIDTH),
        key_up.reshape(WIDTH, HEAD),
        value_up.reshape(WIDTH, HEAD),
    )
    return keys[None, None], values[None, :, None]


def solution(mesh):
    return jax.shard_map(
        shards,
        mesh=mesh,
        in_specs=(
            P(None, ("seq", "tp"), None),
            P(None, ("seq", "tp"), None),
            P(),
            P(None, "tp", None),
            P(None, "tp", None),
        ),
        out_specs=(P("seq", "tp", None, None), P("seq", None, "tp", None)),
        check_vma=False,
    )
```

time: 153 us -> 79.1 us (0.52)
  the two profiles are of different devices: /device:TPU:1 before, /device:TPU:2 now
where the time goes in v1:
time: 79.1 us; the launch traced here: 79 us
  Pallas kernels  73 us (92%)
  local copies, waits for them, and re-layouts  5.33 us (7%)
    pallas_call x1, Pallas kernels, shards(): pl.pallas_call(kernel, out_shape=(jax.ShapeDtypeStruct((HEAD + ROT, lengt...  73 us
    unnamed x4, local copies, waits for them, and re-layouts  5.33 us

profile of v1, /device:TPU:2, one launch (start us, length us, event | category | flops | bytes accessed | tf_op | source)
XLA Modules:
  0.0 79.0 jit_solution(5467683671166930903)
XLA Ops:
  0.6 73.0 %gather_and_expand.1 = (bf16[192,8192]{1,0:T(8,128)(2,1)}, bf16[8192,128]{1,0:T(8,128)(2,1)}) custom-call(bf16[16,32,512]{2,1,0:T(8,128)(2,1)} %lat_ref.1, bf16[16,32,64]{2,1,0:T(8,128)(2,1)} %rot_ref.1, f32[1,512]{1,0:T(1,128)} %bitcast.9, bf16[512,128]{1,0:T(8,128)(2,1)} %bitcast.7, bf16[512,128]{1,0:T(8,128)(2,1)} %bitcast.8), custom_call_target="tpu_custom_call" | custom-call | tf_op jit(solution)/shard_map/gather_and_expand/pallas_call | solution.py:186
  73.6 0.0 copy-start
  73.7 4.0 %copy.9 = bf16[1,1,192,8192]{3,2,1,0:T(8,128)(2,1)} copy(bf16[1,1,192,8192]{3,2,1,0:T(8,128)(2,1)} %bitcast.5) | data formatting | bytes 6291456
  77.7 0.0 copy-done
  77.7 1.3 %copy.10 = bf16[1,8192,1,128]{3,1,2,0:T(8,128)(2,1)} copy(bf16[1,8192,1,128]{3,1,2,0:T(8,128)(2,1)S(1)} %bitcast.6) | data formatting | bytes 4194304
Async XLA Ops:
  73.6 4.0 %copy-start = (bf16[8192,128]{1,0:T(8,128)(2,1)S(1)}, bf16[8192,128]{1,0:T(8,128)(2,1)}, u32[]{:S(2)}) copy-start(bf16[8192,128]{1,0:T(8,128)(2,1)} %get-tuple-element.5) | copy-start | bytes 6291460

commit v2 on v1

--- a/solution.py
+++ b/solution.py
@@ -13,12 +13,13 @@
 CHUNKS = WIDTH // 128
 FLAT = CHUNKS * ROWS
 UNIT = TP * ROWS
-D1, D2, D3, D4 = 1, 2, 3, 5
+D1, D2, D3, D4 = 2, 4, 9, 14
 
 
 def kernel(
-    lat_ref, rot_ref, gain_ref, wk_ref, wv_ref, keys_ref, values_ref,
-    own, held, weights, spread, send_sem, recv_sem,
+    lat_hbm, rot_hbm, gain_hbm, wk_hbm, wv_hbm, keys_ref, values_ref,
+    lat_ref, rot_ref, gain_ref, wk_ref, wv_ref,
+    own, held, weights, spread, load_sem, send_sem, recv_sem,
 ):
     seq, tp = lax.axis_index("seq"), lax.axis_index("tp")
     z, core = seq // 2, seq % 2
@@ -35,6 +36,20 @@
         dx = first_y * q + (1 - first_y) * p
         return ((y + dy + RING) % RING) * RING + (x + dx + RING) % RING
 
+    loads = [
+        pltpu.make_async_copy(source, target, load_sem.at[i])
+        for i, (source, target) in enumerate(
+            (
+                (lat_hbm, lat_ref),
+                (gain_hbm, gain_ref),
+                (rot_hbm, rot_ref),
+                (wk_hbm, wk_ref),
+                (wv_hbm, wv_ref),
+            )
+        )
+    ]
+    for load in loads:
+        load.start()
     barrier = pltpu.get_barrier_semaphore()
 
     def greet(n, _):
@@ -44,6 +59,9 @@
     lax.fori_loop(1, SEQ, greet, 0)
     for p, q in ((1, 0), (-1, 0), (0, 1), (0, -1)):
         pl.semaphore_signal(barrier, inc=1, device_id=(seq, tp_of(0, p, q)))
+
+    for load in loads[:3]:
+        load.wait()
 
     def prepare(s, _):
         rows = lat_ref[s].astype(jnp.float32)
@@ -59,6 +77,8 @@
 
     lax.fori_loop(0, SEQ, prepare, 0)
     held[seq * TP + tp] = own[seq]
+    for load in loads[3:]:
+        load.wait()
     weights[:, :HEAD] = wk_ref[...]
     weights[:, HEAD:] = wv_ref[...]
     row = lax.broadcasted_iota(jnp.int32, (64, 128), 0)
@@ -186,27 +206,38 @@
     keys, values = pl.pallas_call(
         kernel,
         out_shape=(
-            jax.ShapeDtypeStruct((HEAD + ROT, length), jnp.bfloat16),
-            jax.ShapeDtypeStruct((length, HEAD), jnp.bfloat16),
+            pltpu.VMEM((HEAD + ROT, length), jnp.bfloat16),
+            pltpu.VMEM((length, HEAD), jnp.bfloat16),
         ),
-        in_specs=[vmem] * 5,
+        in_specs=[pl.BlockSpec(memory_space=pltpu.HBM)] * 5,
         out_specs=(vmem, vmem),
         scratch_shapes=[
+            pltpu.VMEM((SEQ, ROWS, WIDTH), jnp.bfloat16),
+            pltpu.VMEM((SEQ, ROWS, ROT), jnp.bfloat16),
+            pltpu.VMEM((1, WIDTH), jnp.float32),
+            pltpu.VMEM((WIDTH, HEAD), jnp.bfloat16),
+            pltpu.VMEM((WIDTH, HEAD), jnp.bfloat16),
             pltpu.VMEM((SEQ, PACKED, 128), jnp.bfloat16),
             pltpu.VMEM((SEQ * TP, PACKED, 128), jnp.bfloat16),
             pltpu.VMEM((WIDTH, 2 * HEAD), jnp.bfloat16),
             pltpu.VMEM((2, 64, 128), jnp.bfloat16),
+            pltpu.SemaphoreType.DMA((5,)),
             pltpu.SemaphoreType.DMA,
             pltpu.SemaphoreType.DMA((SEQ * TP,)),
         ],
-        compiler_params=pltpu.CompilerParams(collective_id=0, has_side_effects=True),
+        compiler_params=pltpu.CompilerParams(collective_id=0, has_side_effects=True, vmem_limit_bytes=24 * 2**20),
         name="gather_and_expand",
     )(
-        latents,
-        rotary_rows,
-        latent_gain.reshape(1, WIDTH),
-        key_up.reshape(WIDTH, HEAD),
-        value_up.reshape(WIDTH, HEAD),
+        *(
+            pltpu.with_memory_space_constraint(a, pltpu.HBM)
+            for a in (
+                latents,
+                rotary_rows,
+                latent_gain.reshape(1, WIDTH),
+                key_up.reshape(WIDTH, HEAD),
+                value_up.reshape(WIDTH, HEAD),
+            )
+        )
     )
     return keys[None, None], values[None, :, None]
 

time: 79.1 us -> 68.7 us (0.87)
  the two profiles are of different devices: /device:TPU:2 before, /device:TPU:1 now
where the time goes in v2:
time: 68.7 us; the launch traced here: 68.6 us
  Pallas kernels  65 us (95%)
  local copies, waits for them, and re-layouts  2.99 us (4%)
    pallas_call x1, Pallas kernels, shards(): pl.pallas_call(kernel, out_shape=(pltpu.VMEM((HEAD + ROT, length), jnp.bf...  65 us
    unnamed x2, local copies, waits for them, and re-layouts  2.99 us

profile of v2, /device:TPU:1, one launch (start us, length us, event | category | flops | bytes accessed | tf_op | source)
XLA Modules:
  0.0 68.6 jit_solution(16090314196819763366)
XLA Ops:
  0.6 65.0 %gather_and_expand.1 = (bf16[192,8192]{1,0:T(8,128)(2,1)S(1)}, bf16[8192,128]{1,0:T(8,128)(2,1)S(1)}) custom-call(bf16[16,32,512]{2,1,0:T(8,128)(2,1)} %lat_hbm.1, bf16[16,32,64]{2,1,0:T(8,128)(2,1)} %rot_hbm.1, f32[1,512]{1,0:T(1,128)} %bitcast.9, bf16[512,128]{1,0:T(8,128)(2,1)} %bitcast.7, bf16[512,128]{1,0:T(8,128)(2,1)} %bitcast.8), custom_call_target="tpu_custom_call" | custom-call | tf_op jit(solution)/shard_map/gather_and_expand/pallas_call | solution.py:206
  65.7 1.7 %copy.9 = bf16[1,1,192,8192]{3,2,1,0:T(8,128)(2,1)} copy(bf16[1,1,192,8192]{3,2,1,0:T(8,128)(2,1)S(1)} %bitcast.5) | data formatting | bytes 6291456
  67.3 1.3 %copy.10 = bf16[1,8192,1,128]{3,1,2,0:T(8,128)(2,1)} copy(bf16[1,8192,1,128]{3,1,2,0:T(8,128)(2,1)S(1)} %bitcast.6) | data formatting | bytes 4194304

commit v3 on v2

--- a/solution.py
+++ b/solution.py
@@ -12,14 +12,18 @@
 PACKED = ROWS * WIDTH // 128 + ROWS * ROT // 128
 CHUNKS = WIDTH // 128
 FLAT = CHUNKS * ROWS
+LINE = RING * ROWS
+WIDE = 2 * LINE + RING * (PACKED - FLAT)
 UNIT = TP * ROWS
-D1, D2, D3, D4 = 2, 4, 9, 14
+D1, D2, D3, D4 = 5, 9, 13, 19
+RELAY = 3
 
 
 def kernel(
     lat_hbm, rot_hbm, gain_hbm, wk_hbm, wv_hbm, keys_ref, values_ref,
-    lat_ref, rot_ref, gain_ref, wk_ref, wv_ref,
-    own, held, weights, spread, load_sem, send_sem, recv_sem,
+    lat_ref, rot_ref, gain_ref, own, held, weights, spread,
+    key_rows, rot_rows, wide_out, wide_in,
+    load_sem, send_sem, recv_sem, wide_send, wide_recv, up_send, up_recv,
 ):
     seq, tp = lax.axis_index("seq"), lax.axis_index("tp")
     z, core = seq // 2, seq % 2
@@ -35,6 +39,20 @@
         dy = first_y * p + (1 - first_y) * q
         dx = first_y * q + (1 - first_y) * p
         return ((y + dy + RING) % RING) * RING + (x + dx + RING) % RING
+
+    def line_of(n, q, j):
+        first_y = n % 2
+        at = (first_y * x + (1 - first_y) * y + q + RING) % RING
+        return at * (RING - (RING - 1) * first_y) + j * (1 + (RING - 1) * first_y)
+
+    def up_of(n, q):
+        return 1 + 2 * (1 - n % 2) + (1 - q) // 2
+
+    def way_of(n):
+        return 1 - 2 * ((n // 4) % 2)
+
+    def side_of(n):
+        return 1 - 2 * ((n // 2) % 2)
 
     loads = [
         pltpu.make_async_copy(source, target, load_sem.at[i])
@@ -43,8 +61,8 @@
                 (lat_hbm, lat_ref),
                 (gain_hbm, gain_ref),
                 (rot_hbm, rot_ref),
-                (wk_hbm, wk_ref),
-                (wv_hbm, wv_ref),
+                (wk_hbm, weights.at[0, 0]),
+                (wv_hbm, weights.at[0, 1]),
             )
         )
     ]
@@ -57,8 +75,9 @@
         return _
 
     lax.fori_loop(1, SEQ, greet, 0)
-    for p, q in ((1, 0), (-1, 0), (0, 1), (0, -1)):
-        pl.semaphore_signal(barrier, inc=1, device_id=(seq, tp_of(0, p, q)))
+    around = [tp_of(0, 1, 0), tp_of(0, -1, 0), tp_of(0, 0, 1), tp_of(0, 0, -1)]
+    for target in around:
+        pl.semaphore_signal(barrier, inc=1, device_id=(seq, target))
 
     for load in loads[:3]:
         load.wait()
@@ -79,8 +98,6 @@
     held[seq * TP + tp] = own[seq]
     for load in loads[3:]:
         load.wait()
-    weights[:, :HEAD] = wk_ref[...]
-    weights[:, HEAD:] = wv_ref[...]
     row = lax.broadcasted_iota(jnp.int32, (64, 128), 0)
     lane = lax.broadcasted_iota(jnp.int32, (64, 128), 1)
     for h in range(2):
@@ -101,6 +118,20 @@
 
     lax.fori_loop(1, SEQ, scatter, 0)
 
+    def share(source, target, half, device):
+        return pltpu.make_async_remote_copy(
+            src_ref=weights.at[source, half],
+            dst_ref=weights.at[target, half],
+            send_sem=up_send,
+            recv_sem=up_recv.at[target, half],
+            device_id=device,
+        )
+
+    partner = (z * 2 + 1 - core, tp)
+    for k, target in enumerate(around):
+        back = 1 + k + 1 - 2 * (k % 2)
+        share(0, back, core, (seq, target)).start()
+
     def copy_of(slot, target):
         return pltpu.make_async_remote_copy(
             src_ref=held.at[slot],
@@ -119,6 +150,57 @@
     def send(n, p, q, dp, dq):
         copy_of(slot_of(n, p, q), tp_of(n, dp, dq)).start()
 
+    def wide_copy(n, which, q):
+        return pltpu.make_async_remote_copy(
+            src_ref=wide_out.at[n, which],
+            dst_ref=wide_in.at[n, which],
+            send_sem=wide_send,
+            recv_sem=wide_recv.at[n, which],
+            device_id=(seq, tp_of(n, 0, q)),
+        )
+
+    def times(rows, k):
+        both = jnp.concatenate([weights[k, 0], weights[k, 1]], axis=-1)
+        wide = jnp.dot(rows, both, preferred_element_type=jnp.float32)
+        return wide.astype(jnp.bfloat16)
+
+    def place(n, device, keys, values, rot):
+        key_rows[n, pl.ds(pl.multiple_of(device * ROWS, ROWS), ROWS), :] = keys
+        at = pl.multiple_of(seq_of(n) * UNIT + device * ROWS, ROWS)
+        values_ref[pl.ds(at, ROWS), :] = values
+        rot_rows[n, pl.ds(pl.multiple_of(device * 16, 16), 16), :] = rot
+
+    def expand(n, q, which, target):
+        blocks = [held[seq_of(n) * TP + line_of(n, q, j)] for j in range(RING)]
+        rows = jnp.concatenate(
+            [
+                jnp.concatenate(
+                    [b[c * ROWS : (c + 1) * ROWS] for c in range(CHUNKS)], axis=-1
+                )
+                for b in blocks
+            ],
+            axis=0,
+        )
+        other = times(rows, up_of(n, target))
+        wide_out[n, which, :LINE, :] = other[:, :HEAD]
+        wide_out[n, which, LINE : 2 * LINE, :] = other[:, HEAD:]
+        mine = times(rows, 0)
+        for j, b in enumerate(blocks):
+            at = slice(j * ROWS, (j + 1) * ROWS)
+            wide_out[n, which, 2 * LINE + 16 * j : 2 * LINE + 16 * (j + 1), :] = b[FLAT:]
+            place(n, line_of(n, q, j), mine[at, :HEAD], mine[at, HEAD:], b[FLAT:])
+
+    def finish(n, which, q):
+        for j in range(RING):
+            at = j * ROWS
+            place(
+                n,
+                line_of(n, q, j),
+                wide_in[n, which, at : at + ROWS, :],
+                wide_in[n, which, LINE + at : LINE + at + ROWS, :],
+                wide_in[n, which, 2 * LINE + 16 * j : 2 * LINE + 16 * (j + 1), :],
+            )
+
     def when(n, low=0):
         return pl.when((n >= low) & (n < SEQ))
 
@@ -131,73 +213,78 @@
 
         @when(n0)
         def _():
+            send(n0, 0, 0, 0, side_of(n0))
             send(n0, 0, 0, 1, 0)
             send(n0, 0, 0, -1, 0)
-            send(n0, 0, 0, 0, 1)
-            send(n0, 0, 0, 0, -1)
+
+        @pl.when(it == RELAY)
+        def _():
+            for k in range(1, 5):
+                share(k, k, core, partner).wait_recv()
+                share(k, k, core, partner).start()
 
         @when(n1)
         def _():
-            way = 1 - 2 * ((n1 // 2) % 2)
+            way, side = way_of(n1), side_of(n1)
             arrive(n1, 0 - way, 0)
             send(n1, 0 - way, 0, way, 0)
-            send(n1, 0 - way, 0, 0, 1)
-            send(n1, 0 - way, 0, 0, -1)
+            send(n1, 0 - way, 0, 0, side)
             arrive(n1, way, 0)
-            send(n1, way, 0, 0, 1)
-            send(n1, way, 0, 0, -1)
+            send(n1, way, 0, 0, side)
+
+        @pl.when(it == D2)
+        def _():
+            for k in range(1, 5):
+                share(k, k, 1 - core, partner).wait_recv()
 
         @when(n2)
         def _():
+            side = side_of(n2)
             arrive(n2, 2, 0)
-            send(n2, 2, 0, 0, 1)
-            send(n2, 2, 0, 0, -1)
+            send(n2, 2, 0, 0, side)
+            expand(n2, 0, 0, 0 - side)
 
         @when(n3)
         def _():
-            arrive(n3, 0, -1)
-            send(n3, 0, -1, 0, 1)
-            arrive(n3, -1, 1)
-            send(n3, -1, 1, 0, -1)
-            arrive(n3, 1, -1)
-            send(n3, 1, -1, 0, 1)
-            arrive(n3, 2, 1)
-            send(n3, 2, 1, 0, -1)
+            side = side_of(n3)
+            for p in (0, -1, 1, 2):
+                arrive(n3, p, 0 - side)
+            expand(n3, 0 - side, 1, side)
+
+        @when(n2)
+        def _():
+            wide_copy(n2, 0, 0 - side_of(n2)).start()
 
         @when(n4)
         def _():
-            arrive(n4, 0, 1)
-            arrive(n4, 1, 1)
-            arrive(n4, -1, -1)
-            arrive(n4, 2, -1)
-            for p in (0, -1, 1, 2):
-                arrive(n4, p, 2)
-            u = seq_of(n4)
+            side = side_of(n4)
+            wide_copy(n4, 0, side).wait_recv()
+            wide_copy(n4, 1, side).wait_recv()
+            finish(n4, 0, side)
+            finish(n4, 1, 2)
             for q in range(TP // 4):
-                block = held[pl.ds(u * TP + 4 * q, 4)]
-                rows = jnp.concatenate(
-                    [
-                        block[:, c * ROWS : (c + 1) * ROWS, :].reshape(4 * ROWS, 128)
-                        for c in range(CHUNKS)
-                    ],
-                    axis=-1,
-                )
-                wide = jnp.dot(rows, weights[...], preferred_element_type=jnp.float32)
-                at = pl.multiple_of(u * UNIT + q * 128, 128)
-                values_ref[pl.ds(at, 128), :] = wide[:, HEAD:].astype(jnp.bfloat16)
-                keys_ref[:HEAD, pl.ds(at, 128)] = wide[:, :HEAD].T.astype(jnp.bfloat16)
-                rot = block[:, FLAT:, :].reshape(64, 128).astype(jnp.float32).T
+                at = pl.multiple_of(seq_of(n4) * UNIT + q * 128, 128)
+                part = key_rows[n4, q * 128 : (q + 1) * 128, :].astype(jnp.float32)
+                keys_ref[:HEAD, pl.ds(at, 128)] = part.T.astype(jnp.bfloat16)
+                rot = rot_rows[n4, q * 64 : (q + 1) * 64, :].astype(jnp.float32).T
                 rot = rot.astype(jnp.bfloat16)
                 turned = jnp.dot(
                     rot[:ROT], spread[0], preferred_element_type=jnp.float32
                 ) + jnp.dot(rot[ROT:], spread[1], preferred_element_type=jnp.float32)
                 keys_ref[HEAD:, pl.ds(at, 128)] = turned.astype(jnp.bfloat16)
 
+        @when(n3)
+        def _():
+            wide_copy(n3, 1, side_of(n3)).start()
+
         return carry
 
     lax.fori_loop(0, SEQ + D4, step, 0)
-    sent = SEQ * TP - 1
-    pltpu.make_async_copy(held.at[pl.ds(0, sent)], held.at[pl.ds(0, sent)], send_sem).wait()
+    sent = held.at[pl.ds(0, SEQ - 1 + 7 * SEQ)]
+    pltpu.make_async_copy(sent, sent, send_sem).wait()
+    pltpu.make_async_copy(wide_out, wide_out, wide_send).wait()
+    shared = weights.at[pl.ds(0, 4)]
+    pltpu.make_async_copy(shared, shared, up_send).wait()
 
 
 def shards(latents, rotary_rows, latent_gain, key_up, value_up):
@@ -215,17 +302,25 @@
             pltpu.VMEM((SEQ, ROWS, WIDTH), jnp.bfloat16),
             pltpu.VMEM((SEQ, ROWS, ROT), jnp.bfloat16),
             pltpu.VMEM((1, WIDTH), jnp.float32),
-            pltpu.VMEM((WIDTH, HEAD), jnp.bfloat16),
-            pltpu.VMEM((WIDTH, HEAD), jnp.bfloat16),
             pltpu.VMEM((SEQ, PACKED, 128), jnp.bfloat16),
             pltpu.VMEM((SEQ * TP, PACKED, 128), jnp.bfloat16),
-            pltpu.VMEM((WIDTH, 2 * HEAD), jnp.bfloat16),
+            pltpu.VMEM((5, 2, WIDTH, HEAD), jnp.bfloat16),
             pltpu.VMEM((2, 64, 128), jnp.bfloat16),
+            pltpu.VMEM((SEQ, UNIT, HEAD), jnp.bfloat16),
+            pltpu.VMEM((SEQ, TP * 16, 128), jnp.bfloat16),
+            pltpu.VMEM((SEQ, 2, WIDE, 128), jnp.bfloat16),
+            pltpu.VMEM((SEQ, 2, WIDE, 128), jnp.bfloat16),
             pltpu.SemaphoreType.DMA((5,)),
             pltpu.SemaphoreType.DMA,
             pltpu.SemaphoreType.DMA((SEQ * TP,)),
+            pltpu.SemaphoreType.DMA,
+            pltpu.SemaphoreType.DMA((SEQ, 2)),
+            pltpu.SemaphoreType.DMA,
+            pltpu.SemaphoreType.DMA((5, 2)),
         ],
-        compiler_params=pltpu.CompilerParams(collective_id=0, has_side_effects=True, vmem_limit_bytes=24 * 2**20),
+        compiler_params=pltpu.CompilerParams(
+            collective_id=0, has_side_effects=True, vmem_limit_bytes=40 * 2**20
+        ),
         name="gather_and_expand",
     )(
         *(

time: 68.7 us -> 60.5 us (0.88)
  Pallas kernels: 65 us -> 56.6 us
    pallas_call x1, Pallas kernels: 65 us -> 56.6 us  [shards(): pl.pallas_call(kernel, out_shape=(pltpu.VMEM((HEAD + ROT, length), jnp.bf...]
where the time goes in v3:
time: 60.5 us; the launch traced here: 60.2 us
  Pallas kernels  56.6 us (94%)
  local copies, waits for them, and re-layouts  2.99 us (5%)
  between operations  0.64 us (1%)
    pallas_call x1, Pallas kernels, shards(): pl.pallas_call(kernel, out_shape=(pltpu.VMEM((HEAD + ROT, length), jnp.bf...  56.6 us
    unnamed x2, local copies, waits for them, and re-layouts  2.99 us

profile of v3, /device:TPU:1, one launch (start us, length us, event | category | flops | bytes accessed | tf_op | source)
XLA Modules:
  0.0 60.2 jit_solution(5960687432433007754)
XLA Ops:
  0.6 56.6 %gather_and_expand.1 = (bf16[192,8192]{1,0:T(8,128)(2,1)S(1)}, bf16[8192,128]{1,0:T(8,128)(2,1)S(1)}) custom-call(bf16[16,32,512]{2,1,0:T(8,128)(2,1)} %lat_hbm.1, bf16[16,32,64]{2,1,0:T(8,128)(2,1)} %rot_hbm.1, f32[1,512]{1,0:T(1,128)} %bitcast.9, bf16[512,128]{1,0:T(8,128)(2,1)} %bitcast.7, bf16[512,128]{1,0:T(8,128)(2,1)} %bitcast.8), custom_call_target="tpu_custom_call" | custom-call | tf_op jit(solution)/shard_map/gather_and_expand/pallas_call | solution.py:293
  57.2 1.7 %copy.9 = bf16[1,1,192,8192]{3,2,1,0:T(8,128)(2,1)} copy(bf16[1,1,192,8192]{3,2,1,0:T(8,128)(2,1)S(1)} %bitcast.5) | data formatting | bytes 6291456
  58.9 1.3 %copy.10 = bf16[1,8192,1,128]{3,1,2,0:T(8,128)(2,1)} copy(bf16[1,8192,1,128]{3,1,2,0:T(8,128)(2,1)S(1)} %bitcast.6) | data formatting | bytes 4194304

commit v4 on v3

--- a/solution.py
+++ b/solution.py
@@ -34,6 +34,8 @@
         dz = ((k + 1) // 2) * (1 - 2 * ((k + 1) % 2))
         return ((z + dz + 8) % 8) * 2 + (core + n) % 2
 
+    to_of = seq_of
+
     def tp_of(n, p, q):
         first_y = n % 2
         dy = first_y * p + (1 - first_y) * q
@@ -82,41 +84,28 @@
     for load in loads[:3]:
         load.wait()
 
-    def prepare(s, _):
+    def ready(s):
         rows = lat_ref[s].astype(jnp.float32)
         scale = lax.rsqrt(jnp.mean(rows * rows, axis=-1, keepdims=True) + 1e-06)
-        ready = (rows * scale * gain_ref[...]).astype(jnp.bfloat16)
-        for c in range(CHUNKS):
-            own[s, c * ROWS : (c + 1) * ROWS, :] = ready[:, c * 128 : (c + 1) * 128]
+        rows = (rows * scale * gain_ref[...]).astype(jnp.bfloat16)
         rot = rot_ref[s]
-        own[s, FLAT:PACKED, :] = jnp.concatenate(
-            [rot[: ROWS // 2], rot[ROWS // 2 :]], axis=-1
-        )
-        return _
-
-    lax.fori_loop(0, SEQ, prepare, 0)
-    held[seq * TP + tp] = own[seq]
-    for load in loads[3:]:
-        load.wait()
+        rot = jnp.concatenate([rot[: ROWS // 2], rot[ROWS // 2 :]], axis=-1)
+        return [rows[:, c * 128 : (c + 1) * 128] for c in range(CHUNKS)] + [rot]
+
+    def put(ref, at, parts):
+        for c, part in enumerate(parts):
+            ref[at, c * ROWS : c * ROWS + part.shape[0], :] = part
+
+    put(held, seq * TP + tp, ready(seq))
     row = lax.broadcasted_iota(jnp.int32, (64, 128), 0)
     lane = lax.broadcasted_iota(jnp.int32, (64, 128), 1)
     for h in range(2):
         at = (row // 16) * 32 + h * 16 + row % 16
         spread[h] = (at == lane).astype(jnp.float32).astype(jnp.bfloat16)
+    for load in loads[3:]:
+        load.wait()
 
     pl.semaphore_wait(barrier, SEQ - 1 + 4)
-
-    def scatter(n, _):
-        pltpu.make_async_remote_copy(
-            src_ref=own.at[seq_of(n)],
-            dst_ref=held.at[seq * TP + tp],
-            send_sem=send_sem,
-            recv_sem=recv_sem.at[seq * TP + tp],
-            device_id=(seq_of(n), tp),
-        ).start()
-        return _
-
-    lax.fori_loop(1, SEQ, scatter, 0)
 
     def share(source, target, half, device):
         return pltpu.make_async_remote_copy(
@@ -201,6 +190,34 @@
                 wide_in[n, which, 2 * LINE + 16 * j : 2 * LINE + 16 * (j + 1), :],
             )
 
+    def scatter(n):
+        pltpu.make_async_remote_copy(
+            src_ref=own.at[to_of(n)],
+            dst_ref=held.at[seq * TP + tp],
+            send_sem=send_sem,
+            recv_sem=recv_sem.at[seq * TP + tp],
+            device_id=(to_of(n), tp),
+        ).start()
+
+    def first(n):
+        send(n, 0, 0, 0, side_of(n))
+        send(n, 0, 0, 1, 0)
+        send(n, 0, 0, -1, 0)
+
+    first(0)
+
+    def prepare(n, _):
+        put(own, to_of(n), ready(to_of(n)))
+
+        @pl.when(n > 1)
+        def _send():
+            scatter(n - 1)
+
+        return _
+
+    lax.fori_loop(1, SEQ, prepare, 0)
+    scatter(SEQ - 1)
+
     def when(n, low=0):
         return pl.when((n >= low) & (n < SEQ))
 
@@ -210,12 +227,7 @@
         @when(n0, 1)
         def _():
             arrive(n0, 0, 0)
-
-        @when(n0)
-        def _():
-            send(n0, 0, 0, 0, side_of(n0))
-            send(n0, 0, 0, 1, 0)
-            send(n0, 0, 0, -1, 0)
+            first(n0)
 
         @pl.when(it == RELAY)
         def _():
@@ -243,6 +255,7 @@
             arrive(n2, 2, 0)
             send(n2, 2, 0, 0, side)
             expand(n2, 0, 0, 0 - side)
+            wide_copy(n2, 0, 0 - side).start()
 
         @when(n3)
         def _():
@@ -250,10 +263,7 @@
             for p in (0, -1, 1, 2):
                 arrive(n3, p, 0 - side)
             expand(n3, 0 - side, 1, side)
-
-        @when(n2)
-        def _():
-            wide_copy(n2, 0, 0 - side_of(n2)).start()
+            wide_copy(n3, 1, side).start()
 
         @when(n4)
         def _():
@@ -273,10 +283,6 @@
                 ) + jnp.dot(rot[ROT:], spread[1], preferred_element_type=jnp.float32)
                 keys_ref[HEAD:, pl.ds(at, 128)] = turned.astype(jnp.bfloat16)
 
-        @when(n3)
-        def _():
-            wide_copy(n3, 1, side_of(n3)).start()
-
         return carry
 
     lax.fori_loop(0, SEQ + D4, step, 0)
@@ -285,6 +291,22 @@
     pltpu.make_async_copy(wide_out, wide_out, wide_send).wait()
     shared = weights.at[pl.ds(0, 4)]
     pltpu.make_async_copy(shared, shared, up_send).wait()
+
+
+def store(keys_ref, values_ref, keys_out, values_out, sem):
+    copies = []
+    for i in range(8):
+        rows = pl.ds(24 * i, 24)
+        copies.append(pltpu.make_async_copy(keys_ref.at[rows], keys_out.at[rows], sem.at[i]))
+    for i in range(8):
+        rows = pl.ds(1024 * i, 1024)
+        copies.append(
+            pltpu.make_async_copy(values_ref.at[rows], values_out.at[rows], sem.at[8 + i])
+        )
+    for copy in copies:
+        copy.start()
+    for copy in copies:
+        copy.wait()
 
 
 def shards(latents, rotary_rows, latent_gain, key_up, value_up):
@@ -334,6 +356,19 @@
             )
         )
     )
+    hbm = pl.BlockSpec(memory_space=pltpu.HBM)
+    keys, values = pl.pallas_call(
+        store,
+        out_shape=(
+            jax.ShapeDtypeStruct(keys.shape, keys.dtype),
+            jax.ShapeDtypeStruct(values.shape, values.dtype),
+        ),
+        in_specs=[vmem, vmem],
+        out_specs=(hbm, hbm),
+        scratch_shapes=[pltpu.SemaphoreType.DMA((16,))],
+        compiler_params=pltpu.CompilerParams(vmem_limit_bytes=2**20),
+        name="store",
+    )(keys, values)
     return keys[None, None], values[None, :, None]
 
 

time: 60.5 us -> 59.7 us (0.987)
  local copies, waits for them, and re-layouts: 2.99 us -> 0 us
  Pallas kernels: 56.6 us -> 58.9 us
    unnamed x2 -> x0, local copies, waits for them, and re-layouts: 2.99 us -> none
    pallas_call x0 -> x1, Pallas kernels: none -> 2.46 us  [shards(): pl.pallas_call(store, out_shape=(jax.ShapeDtypeStruct(keys.shape, keys.dt...]
where the time goes in v4:
time: 59.7 us; the launch traced here: 59.6 us
  Pallas kernels  58.9 us (99%)
  between operations  0.64 us (1%)
    pallas_call x1, Pallas kernels, shards(): pl.pallas_call(kernel, out_shape=(pltpu.VMEM((HEAD + ROT, length), jnp.bf...  56.5 us
    pallas_call x1, Pallas kernels, shards(): pl.pallas_call(store, out_shape=(jax.ShapeDtypeStruct(keys.shape, keys.dt...  2.46 us

profile of v4, /device:TPU:1, one launch (start us, length us, event | category | flops | bytes accessed | tf_op | source)
XLA Modules:
  0.0 59.6 jit_solution(15847300273204193367)
XLA Ops:
  0.6 56.5 %gather_and_expand.1 = (bf16[192,8192]{1,0:T(8,128)(2,1)S(1)}, bf16[8192,128]{1,0:T(8,128)(2,1)S(1)}) custom-call(bf16[16,32,512]{2,1,0:T(8,128)(2,1)} %lat_hbm.1, bf16[16,32,64]{2,1,0:T(8,128)(2,1)} %rot_hbm.1, f32[1,512]{1,0:T(1,128)} %bitcast.7, bf16[512,128]{1,0:T(8,128)(2,1)} %bitcast.5, bf16[512,128]{1,0:T(8,128)(2,1)} %bitcast.6), custom_call_target="tpu_custom_call" | custom-call | tf_op jit(solution)/shard_map/gather_and_expand/pallas_call | solution.py:315
  57.1 2.5 %store.1 = (bf16[192,8192]{1,0:T(8,128)(2,1)}, bf16[8192,128]{1,0:T(8,128)(2,1)}) custom-call(bf16[192,8192]{1,0:T(8,128)(2,1)S(1)} %get-tuple-element.6.keys_ref, bf16[8192,128]{1,0:T(8,128)(2,1)S(1)} %get-tuple-element.7.values_ref), custom_call_target="tpu_custom_call" | custom-call | tf_op jit(solution)/shard_map/store/pallas_call | solution.py:360

commit v5 on v4

--- a/solution.py
+++ b/solution.py
@@ -15,7 +15,7 @@
 LINE = RING * ROWS
 WIDE = 2 * LINE + RING * (PACKED - FLAT)
 UNIT = TP * ROWS
-D1, D2, D3, D4 = 5, 9, 13, 19
+D1, D2, D3, D4 = 4, 8, 12, 18
 RELAY = 3
 
 
@@ -23,7 +23,8 @@
     lat_hbm, rot_hbm, gain_hbm, wk_hbm, wv_hbm, keys_ref, values_ref,
     lat_ref, rot_ref, gain_ref, own, held, weights, spread,
     key_rows, rot_rows, wide_out, wide_in,
-    load_sem, send_sem, recv_sem, wide_send, wide_recv, up_send, up_recv,
+    load_sem, send_sem, first_recv, near_recv, far_recv, line_recv,
+    wide_send, wide_recv, up_send, up_recv,
 ):
     seq, tp = lax.axis_index("seq"), lax.axis_index("tp")
     z, core = seq // 2, seq % 2
@@ -57,7 +58,7 @@
         return 1 - 2 * ((n // 2) % 2)
 
     loads = [
-        pltpu.make_async_copy(source, target, load_sem.at[i])
+        pltpu.make_async_copy(source, target, load_sem.at[min(i, 3)])
         for i, (source, target) in enumerate(
             (
                 (lat_hbm, lat_ref),
@@ -102,49 +103,51 @@
     for h in range(2):
         at = (row // 16) * 32 + h * 16 + row % 16
         spread[h] = (at == lane).astype(jnp.float32).astype(jnp.bfloat16)
-    for load in loads[3:]:
-        load.wait()
+    pltpu.make_async_copy(weights.at[0], weights.at[0], load_sem.at[3]).wait()
 
     pl.semaphore_wait(barrier, SEQ - 1 + 4)
 
-    def share(source, target, half, device):
+    def share(source, target, half, device, recv_sem):
         return pltpu.make_async_remote_copy(
             src_ref=weights.at[source, half],
             dst_ref=weights.at[target, half],
             send_sem=up_send,
-            recv_sem=up_recv.at[target, half],
+            recv_sem=recv_sem,
             device_id=device,
         )
+
+    def shared(recv_sem):
+        part = weights.at[pl.ds(1, 2)]
+        pltpu.make_async_copy(part, part, recv_sem).wait()
 
     partner = (z * 2 + 1 - core, tp)
     for k, target in enumerate(around):
         back = 1 + k + 1 - 2 * (k % 2)
-        share(0, back, core, (seq, target)).start()
-
-    def copy_of(slot, target):
-        return pltpu.make_async_remote_copy(
+        share(0, back, core, (seq, target), up_recv.at[0]).start()
+
+    def slot_of(n, p, q):
+        return seq_of(n) * TP + tp_of(n, p, q)
+
+    def arrive(recv_sem, blocks):
+        part = held.at[pl.ds(0, blocks)]
+        pltpu.make_async_copy(part, part, recv_sem).wait()
+
+    def send(n, p, q, dp, dq, recv_sem):
+        slot = slot_of(n, p, q)
+        pltpu.make_async_remote_copy(
             src_ref=held.at[slot],
             dst_ref=held.at[slot],
             send_sem=send_sem,
-            recv_sem=recv_sem.at[slot],
-            device_id=(seq, target),
-        )
-
-    def slot_of(n, p, q):
-        return seq_of(n) * TP + tp_of(n, p, q)
-
-    def arrive(n, p, q):
-        copy_of(slot_of(n, p, q), tp_of(n, 1, 0)).wait_recv()
-
-    def send(n, p, q, dp, dq):
-        copy_of(slot_of(n, p, q), tp_of(n, dp, dq)).start()
+            recv_sem=recv_sem.at[n],
+            device_id=(seq, tp_of(n, dp, dq)),
+        ).start()
 
     def wide_copy(n, which, q):
         return pltpu.make_async_remote_copy(
             src_ref=wide_out.at[n, which],
             dst_ref=wide_in.at[n, which],
             send_sem=wide_send,
-            recv_sem=wide_recv.at[n, which],
+            recv_sem=wide_recv.at[n],
             device_id=(seq, tp_of(n, 0, q)),
         )
 
@@ -195,14 +198,14 @@
             src_ref=own.at[to_of(n)],
             dst_ref=held.at[seq * TP + tp],
             send_sem=send_sem,
-            recv_sem=recv_sem.at[seq * TP + tp],
+            recv_sem=first_recv.at[seq],
             device_id=(to_of(n), tp),
         ).start()
 
     def first(n):
-        send(n, 0, 0, 0, side_of(n))
-        send(n, 0, 0, 1, 0)
-        send(n, 0, 0, -1, 0)
+        send(n, 0, 0, 0, side_of(n), line_recv)
+        send(n, 0, 0, 1, 0, near_recv)
+        send(n, 0, 0, -1, 0, near_recv)
 
     first(0)
 
@@ -226,50 +229,46 @@
 
         @when(n0, 1)
         def _():
-            arrive(n0, 0, 0)
+            arrive(first_recv.at[seq_of(n0)], 1)
             first(n0)
 
         @pl.when(it == RELAY)
         def _():
+            shared(up_recv.at[0])
             for k in range(1, 5):
-                share(k, k, core, partner).wait_recv()
-                share(k, k, core, partner).start()
+                share(k, k, core, partner, up_recv.at[1]).start()
 
         @when(n1)
         def _():
             way, side = way_of(n1), side_of(n1)
-            arrive(n1, 0 - way, 0)
-            send(n1, 0 - way, 0, way, 0)
-            send(n1, 0 - way, 0, 0, side)
-            arrive(n1, way, 0)
-            send(n1, way, 0, 0, side)
+            arrive(near_recv.at[n1], 2)
+            send(n1, 0 - way, 0, way, 0, far_recv)
+            send(n1, 0 - way, 0, 0, side, line_recv)
+            send(n1, way, 0, 0, side, line_recv)
 
         @pl.when(it == D2)
         def _():
-            for k in range(1, 5):
-                share(k, k, 1 - core, partner).wait_recv()
+            shared(up_recv.at[1])
 
         @when(n2)
         def _():
             side = side_of(n2)
-            arrive(n2, 2, 0)
-            send(n2, 2, 0, 0, side)
+            arrive(far_recv.at[n2], 1)
+            send(n2, 2, 0, 0, side, line_recv)
             expand(n2, 0, 0, 0 - side)
             wide_copy(n2, 0, 0 - side).start()
 
         @when(n3)
         def _():
             side = side_of(n3)
-            for p in (0, -1, 1, 2):
-                arrive(n3, p, 0 - side)
+            arrive(line_recv.at[n3], 4)
             expand(n3, 0 - side, 1, side)
             wide_copy(n3, 1, side).start()
 
         @when(n4)
         def _():
             side = side_of(n4)
-            wide_copy(n4, 0, side).wait_recv()
-            wide_copy(n4, 1, side).wait_recv()
+            pltpu.make_async_copy(wide_in.at[n4], wide_in.at[n4], wide_recv.at[n4]).wait()
             finish(n4, 0, side)
             finish(n4, 1, 2)
             for q in range(TP // 4):
@@ -289,8 +288,8 @@
     sent = held.at[pl.ds(0, SEQ - 1 + 7 * SEQ)]
     pltpu.make_async_copy(sent, sent, send_sem).wait()
     pltpu.make_async_copy(wide_out, wide_out, wide_send).wait()
-    shared = weights.at[pl.ds(0, 4)]
-    pltpu.make_async_copy(shared, shared, up_send).wait()
+    given = weights.at[pl.ds(0, 4)]
+    pltpu.make_async_copy(given, given, up_send).wait()
 
 
 def store(keys_ref, values_ref, keys_out, values_out, sem):
@@ -332,13 +331,16 @@
             pltpu.VMEM((SEQ, TP * 16, 128), jnp.bfloat16),
             pltpu.VMEM((SEQ, 2, WIDE, 128), jnp.bfloat16),
             pltpu.VMEM((SEQ, 2, WIDE, 128), jnp.bfloat16),
-            pltpu.SemaphoreType.DMA((5,)),
+            pltpu.SemaphoreType.DMA((4,)),
             pltpu.SemaphoreType.DMA,
-            pltpu.SemaphoreType.DMA((SEQ * TP,)),
+            pltpu.SemaphoreType.DMA((SEQ,)),
+            pltpu.SemaphoreType.DMA((SEQ,)),
+            pltpu.SemaphoreType.DMA((SEQ,)),
+            pltpu.SemaphoreType.DMA((SEQ,)),
             pltpu.SemaphoreType.DMA,
-            pltpu.SemaphoreType.DMA((SEQ, 2)),
+            pltpu.SemaphoreType.DMA((SEQ,)),
             pltpu.SemaphoreType.DMA,
-            pltpu.SemaphoreType.DMA((5, 2)),
+            pltpu.SemaphoreType.DMA((2,)),
         ],
         compiler_params=pltpu.CompilerParams(
             collective_id=0, has_side_effects=True, vmem_limit_bytes=40 * 2**20

time: 59.7 us -> 57.7 us (0.966)
  Pallas kernels: 58.9 us -> 56.5 us
    pallas_call x1, Pallas kernels: 56.5 us -> 54.1 us  [shards(): pl.pallas_call(kernel, out_shape=(pltpu.VMEM((HEAD + ROT, length), jnp.bf...]
where the time goes in v5:
time: 57.7 us; the launch traced here: 57.2 us
  Pallas kernels  56.5 us (98%)
  between operations  0.64 us (1%)
    pallas_call x1, Pallas kernels, shards(): pl.pallas_call(kernel, out_shape=(pltpu.VMEM((HEAD + ROT, length), jnp.bf...  54.1 us
    pallas_call x1, Pallas kernels, shards(): pl.pallas_call(store, out_shape=(jax.ShapeDtypeStruct(keys.shape, keys.dt...  2.46 us

profile of v5, /device:TPU:1, one launch (start us, length us, event | category | flops | bytes accessed | tf_op | source)
XLA Modules:
  0.0 57.2 jit_solution(5198522745203812882)
XLA Ops:
  0.6 54.1 %gather_and_expand.1 = (bf16[192,8192]{1,0:T(8,128)(2,1)S(1)}, bf16[8192,128]{1,0:T(8,128)(2,1)S(1)}) custom-call(bf16[16,32,512]{2,1,0:T(8,128)(2,1)} %lat_hbm.1, bf16[16,32,64]{2,1,0:T(8,128)(2,1)} %rot_hbm.1, f32[1,512]{1,0:T(1,128)} %bitcast.7, bf16[512,128]{1,0:T(8,128)(2,1)} %bitcast.5, bf16[512,128]{1,0:T(8,128)(2,1)} %bitcast.6), custom_call_target="tpu_custom_call" | custom-call | tf_op jit(solution)/shard_map/gather_and_expand/pallas_call | solution.py:314
  54.7 2.5 %store.1 = (bf16[192,8192]{1,0:T(8,128)(2,1)}, bf16[8192,128]{1,0:T(8,128)(2,1)}) custom-call(bf16[192,8192]{1,0:T(8,128)(2,1)S(1)} %get-tuple-element.6.keys_ref, bf16[8192,128]{1,0:T(8,128)(2,1)S(1)} %get-tuple-element.7.values_ref), custom_call_target="tpu_custom_call" | custom-call | tf_op jit(solution)/shard_map/store/pallas_call | solution.py:362

commit v6 on v5

--- a/solution.py
+++ b/solution.py
@@ -17,13 +17,14 @@
 UNIT = TP * ROWS
 D1, D2, D3, D4 = 4, 8, 12, 18
 RELAY = 3
+NEAR = 10
 
 
 def kernel(
     lat_hbm, rot_hbm, gain_hbm, wk_hbm, wv_hbm, keys_ref, values_ref,
     lat_ref, rot_ref, gain_ref, own, held, weights, spread,
     key_rows, rot_rows, wide_out, wide_in,
-    load_sem, send_sem, first_recv, near_recv, far_recv, line_recv,
+    past_sem, load_sem, send_sem, first_recv, near_recv, far_recv, line_recv,
     wide_send, wide_recv, up_send, up_recv,
 ):
     seq, tp = lax.axis_index("seq"), lax.axis_index("tp")
@@ -77,7 +78,7 @@
         pl.semaphore_signal(barrier, inc=1, device_id=(seq_of(n), tp))
         return _
 
-    lax.fori_loop(1, SEQ, greet, 0)
+    lax.fori_loop(1, NEAR, greet, 0)
     around = [tp_of(0, 1, 0), tp_of(0, -1, 0), tp_of(0, 0, 1), tp_of(0, 0, -1)]
     for target in around:
         pl.semaphore_signal(barrier, inc=1, device_id=(seq, target))
@@ -105,7 +106,11 @@
         spread[h] = (at == lane).astype(jnp.float32).astype(jnp.bfloat16)
     pltpu.make_async_copy(weights.at[0], weights.at[0], load_sem.at[3]).wait()
 
-    pl.semaphore_wait(barrier, SEQ - 1 + 4)
+    pl.semaphore_wait(barrier, NEAR - 1 + 4)
+    for dz in (2, 6):
+        pl.semaphore_signal(
+            past_sem, inc=1, device_id=(((z + dz) % 8) * 2 + core, tp)
+        )
 
     def share(source, target, half, device, recv_sem):
         return pltpu.make_async_remote_copy(
@@ -212,13 +217,16 @@
     def prepare(n, _):
         put(own, to_of(n), ready(to_of(n)))
 
-        @pl.when(n > 1)
+        @pl.when((n > 1) & (n != NEAR))
         def _send():
             scatter(n - 1)
 
         return _
 
-    lax.fori_loop(1, SEQ, prepare, 0)
+    lax.fori_loop(1, NEAR, prepare, 0)
+    scatter(NEAR - 1)
+    pl.semaphore_wait(past_sem, 2)
+    lax.fori_loop(NEAR, SEQ, prepare, 0)
     scatter(SEQ - 1)
 
     def when(n, low=0):
@@ -331,6 +339,7 @@
             pltpu.VMEM((SEQ, TP * 16, 128), jnp.bfloat16),
             pltpu.VMEM((SEQ, 2, WIDE, 128), jnp.bfloat16),
             pltpu.VMEM((SEQ, 2, WIDE, 128), jnp.bfloat16),
+            pltpu.SemaphoreType.REGULAR,
             pltpu.SemaphoreType.DMA((4,)),
             pltpu.SemaphoreType.DMA,
             pltpu.SemaphoreType.DMA((SEQ,)),

time: 57.7 us -> 56.7 us (0.983)
  Pallas kernels: 56.5 us -> 55.5 us
    pallas_call x1, Pallas kernels: 54.1 us -> 53 us  [shards(): pl.pallas_call(kernel, out_shape=(pltpu.VMEM((HEAD + ROT, length), jnp.bf...]
where the time goes in v6:
time: 56.7 us; the launch traced here: 56.1 us
  Pallas kernels  55.5 us (98%)
  between operations  0.64 us (1%)
    pallas_call x1, Pallas kernels, shards(): pl.pallas_call(kernel, out_shape=(pltpu.VMEM((HEAD + ROT, length), jnp.bf...  53 us
    pallas_call x1, Pallas kernels, shards(): pl.pallas_call(store, out_shape=(jax.ShapeDtypeStruct(keys.shape, keys.dt...  2.46 us

profile of v6, /device:TPU:1, one launch (start us, length us, event | category | flops | bytes accessed | tf_op | source)
XLA Modules:
  0.0 56.1 jit_solution(5444419289038312189)
XLA Ops:
  0.6 53.0 %gather_and_expand.1 = (bf16[192,8192]{1,0:T(8,128)(2,1)S(1)}, bf16[8192,128]{1,0:T(8,128)(2,1)S(1)}) custom-call(bf16[16,32,512]{2,1,0:T(8,128)(2,1)} %lat_hbm.1, bf16[16,32,64]{2,1,0:T(8,128)(2,1)} %rot_hbm.1, f32[1,512]{1,0:T(1,128)} %bitcast.7, bf16[512,128]{1,0:T(8,128)(2,1)} %bitcast.5, bf16[512,128]{1,0:T(8,128)(2,1)} %bitcast.6), custom_call_target="tpu_custom_call" | custom-call | tf_op jit(solution)/shard_map/gather_and_expand/pallas_call | solution.py:322
  53.7 2.5 %store.1 = (bf16[192,8192]{1,0:T(8,128)(2,1)}, bf16[8192,128]{1,0:T(8,128)(2,1)}) custom-call(bf16[192,8192]{1,0:T(8,128)(2,1)S(1)} %get-tuple-element.6.keys_ref, bf16[8192,128]{1,0:T(8,128)(2,1)S(1)} %get-tuple-element.7.values_ref), custom_call_target="tpu_custom_call" | custom-call | tf_op jit(solution)/shard_map/store/pallas_call | solution.py:371

commit v7 on v6

--- a/solution.py
+++ b/solution.py
@@ -17,6 +17,7 @@
 UNIT = TP * ROWS
 D1, D2, D3, D4 = 4, 8, 12, 18
 RELAY = 3
+AHEAD = 9
 NEAR = 10
 
 
@@ -106,6 +107,11 @@
         spread[h] = (at == lane).astype(jnp.float32).astype(jnp.bfloat16)
     pltpu.make_async_copy(weights.at[0], weights.at[0], load_sem.at[3]).wait()
 
+    def put_own(n, _):
+        put(own, to_of(n), ready(to_of(n)))
+        return _
+
+    lax.fori_loop(1, AHEAD, put_own, 0)
     pl.semaphore_wait(barrier, NEAR - 1 + 4)
     for dz in (2, 6):
         pl.semaphore_signal(
@@ -223,7 +229,9 @@
 
         return _
 
-    lax.fori_loop(1, NEAR, prepare, 0)
+    for n in range(1, AHEAD - 1):
+        scatter(n)
+    lax.fori_loop(AHEAD, NEAR, prepare, 0)
     scatter(NEAR - 1)
     pl.semaphore_wait(past_sem, 2)
     lax.fori_loop(NEAR, SEQ, prepare, 0)

time: 56.7 us -> 56.7 us (level)
  no operation moved by 1% of the time
where the time goes in v7:
time: 56.7 us; the launch traced here: 56.3 us
  Pallas kernels  55.7 us (98%)
  between operations  0.64 us (1%)
    pallas_call x1, Pallas kernels, shards(): pl.pallas_call(kernel, out_shape=(pltpu.VMEM((HEAD + ROT, length), jnp.bf...  53.2 us
    pallas_call x1, Pallas kernels, shards(): pl.pallas_call(store, out_shape=(jax.ShapeDtypeStruct(keys.shape, keys.dt...  2.46 us

profile of v7, /device:TPU:1, one launch (start us, length us, event | category | flops | bytes accessed | tf_op | source)
XLA Modules:
  0.0 56.3 jit_solution(15431631895509280193)
XLA Ops:
  0.6 53.2 %gather_and_expand.1 = (bf16[192,8192]{1,0:T(8,128)(2,1)S(1)}, bf16[8192,128]{1,0:T(8,128)(2,1)S(1)}) custom-call(bf16[16,32,512]{2,1,0:T(8,128)(2,1)} %lat_hbm.1, bf16[16,32,64]{2,1,0:T(8,128)(2,1)} %rot_hbm.1, f32[1,512]{1,0:T(1,128)} %bitcast.7, bf16[512,128]{1,0:T(8,128)(2,1)} %bitcast.5, bf16[512,128]{1,0:T(8,128)(2,1)} %bitcast.6), custom_call_target="tpu_custom_call" | custom-call | tf_op jit(solution)/shard_map/gather_and_expand/pallas_call | solution.py:330
  53.9 2.5 %store.1 = (bf16[192,8192]{1,0:T(8,128)(2,1)}, bf16[8192,128]{1,0:T(8,128)(2,1)}) custom-call(bf16[192,8192]{1,0:T(8,128)(2,1)S(1)} %get-tuple-element.6.keys_ref, bf16[8192,128]{1,0:T(8,128)(2,1)S(1)} %get-tuple-element.7.values_ref), custom_call_target="tpu_custom_call" | custom-call | tf_op jit(solution)/shard_map/store/pallas_call | solution.py:379

commit v8 on v6

--- a/solution.py
+++ b/solution.py
@@ -15,8 +15,8 @@
 LINE = RING * ROWS
 WIDE = 2 * LINE + RING * (PACKED - FLAT)
 UNIT = TP * ROWS
-D1, D2, D3, D4 = 4, 8, 12, 18
-RELAY = 3
+D1, D2, D3, D4 = 4, 8, 12, 17
+RELAY = 5
 NEAR = 10
 
 
@@ -203,7 +203,7 @@
             src_ref=own.at[to_of(n)],
             dst_ref=held.at[seq * TP + tp],
             send_sem=send_sem,
-            recv_sem=first_recv.at[seq],
+            recv_sem=first_recv.at[z],
             device_id=(to_of(n), tp),
         ).start()
 
@@ -235,9 +235,16 @@
     def step(it, carry):
         n0, n1, n2, n3, n4 = it, it - D1, it - D2, it - D3, it - D4
 
+        @pl.when(n0 == 1)
+        def _():
+            arrive(first_recv.at[z], 1)
+
+        @pl.when((n0 > 1) & (n0 < SEQ) & (n0 % 2 == 0))
+        def _():
+            arrive(first_recv.at[seq_of(n0) // 2], 2)
+
         @when(n0, 1)
         def _():
-            arrive(first_recv.at[seq_of(n0)], 1)
             first(n0)
 
         @pl.when(it == RELAY)
@@ -342,7 +349,7 @@
             pltpu.SemaphoreType.REGULAR,
             pltpu.SemaphoreType.DMA((4,)),
             pltpu.SemaphoreType.DMA,
-            pltpu.SemaphoreType.DMA((SEQ,)),
+            pltpu.SemaphoreType.DMA((SEQ // 2,)),
             pltpu.SemaphoreType.DMA((SEQ,)),
             pltpu.SemaphoreType.DMA((SEQ,)),
             pltpu.SemaphoreType.DMA((SEQ,)),

time: 56.7 us -> 58.1 us (1.025)
  Pallas kernels: 55.5 us -> 57.3 us
    pallas_call x1, Pallas kernels: 53 us -> 54.9 us  [shards(): pl.pallas_call(kernel, out_shape=(pltpu.VMEM((HEAD + ROT, length), jnp.bf...]
where the time goes in v8:
time: 58.1 us; the launch traced here: 58 us
  Pallas kernels  57.3 us (99%)
  between operations  0.64 us (1%)
    pallas_call x1, Pallas kernels, shards(): pl.pallas_call(kernel, out_shape=(pltpu.VMEM((HEAD + ROT, length), jnp.bf...  54.9 us
    pallas_call x1, Pallas kernels, shards(): pl.pallas_call(store, out_shape=(jax.ShapeDtypeStruct(keys.shape, keys.dt...  2.46 us

profile of v8, /device:TPU:1, one launch (start us, length us, event | category | flops | bytes accessed | tf_op | source)
XLA Modules:
  0.0 58.0 jit_solution(17626254102652148247)
XLA Ops:
  0.6 54.9 %gather_and_expand.1 = (bf16[192,8192]{1,0:T(8,128)(2,1)S(1)}, bf16[8192,128]{1,0:T(8,128)(2,1)S(1)}) custom-call(bf16[16,32,512]{2,1,0:T(8,128)(2,1)} %lat_hbm.1, bf16[16,32,64]{2,1,0:T(8,128)(2,1)} %rot_hbm.1, f32[1,512]{1,0:T(1,128)} %bitcast.7, bf16[512,128]{1,0:T(8,128)(2,1)} %bitcast.5, bf16[512,128]{1,0:T(8,128)(2,1)} %bitcast.6), custom_call_target="tpu_custom_call" | custom-call | tf_op jit(solution)/shard_map/gather_and_expand/pallas_call | solution.py:329
  55.5 2.5 %store.1 = (bf16[192,8192]{1,0:T(8,128)(2,1)}, bf16[8192,128]{1,0:T(8,128)(2,1)}) custom-call(bf16[192,8192]{1,0:T(8,128)(2,1)S(1)} %get-tuple-element.6.keys_ref, bf16[8192,128]{1,0:T(8,128)(2,1)S(1)} %get-tuple-element.7.values_ref), custom_call_target="tpu_custom_call" | custom-call | tf_op jit(solution)/shard_map/store/pallas_call | solution.py:378
